TPU v7x, 256 devices: a whole 4x4x8 slice. The times are simulated.
256 devices in a mesh: fsdp: 32 (over z, y), rep: 8 (over x, core).
Axes of the slice: x: 4, y: 4, z: 8, core: 2. Of those that a mesh axis runs over, the one named last changes fastest.
Arguments:
- hidden: bfloat16 [65536, 2048], P(('fsdp', 'rep')), may hold values from -6 to 6
- attn_gain: bfloat16 [2048], P(('fsdp', 'rep')), may hold values from 0.25 to 1.75
- w_query: bfloat16 [2048, 2048], P(('fsdp', 'rep')), as said below
- w_key: bfloat16 [2048, 512], P(('fsdp', 'rep')), as said below
- w_value: bfloat16 [2048, 512], P(('fsdp', 'rep')), may hold values from -0.125 to 0.125
- w_out: bfloat16 [2048, 2048], P(None, ('fsdp', 'rep')), may hold values from -0.125 to 0.125
Outputs:
- mixed: bfloat16 [65536, 2048], P(('fsdp', 'rep'))
Inputs may be any that keep to these rules, and one draw needn't show every extreme that they name: `w_query`: entries of order 2048^(-1/2). `w_key`: entries of order 2048^(-1/2) times a factor up to twenty.
All inputs are finite; a program needn't handle non-finite values.
Results may differ from a plain program's by a relative error of at most 0.012.
The roundings to bfloat16 on the way count: a program that leaves them out, or rounds other values in their place, can miss the bound.
Values may be sent and summed in bfloat16 or wider, within the bound.
A program may use at most 64 MiB of HBM per device.

v0:
```python
import jax
import jax.numpy as jnp
from jax import lax
from jax.sharding import PartitionSpec as P

HD = 64
rope_base = 500000.0
norm_eps = 1e-05


def sent_together(arrays, axis, dim, along):
    columns = [a.reshape(*a.shape[:along], -1) for a in arrays]
    both = jnp.concatenate(columns, axis=along)
    filled, at, gathered = (lax.all_gather(both, axis, axis=dim, tiled=True), 0, [])
    for a, column in zip(arrays, columns):
        piece = filled[..., at : at + column.shape[along]]
        gathered.append(piece.reshape(*piece.shape[:along], *a.shape[along:]))
        at += column.shape[along]
    return tuple(gathered)


def copy_for_each(array, axis):
    copies = jnp.broadcast_to(array, (lax.axis_size(axis), *array.shape))
    return lax.all_to_all(copies, axis, split_axis=0, concat_axis=0, tiled=True)


def laid_out(blocks, dim):
    blocks = jnp.moveaxis(blocks, 0, dim)
    dims = blocks.shape
    return blocks.reshape(*dims[:dim], dims[dim] * dims[dim + 1], *dims[dim + 2 :])


def gather_directly(array, axis, dim):
    blocks = copy_for_each(array, axis)
    return laid_out(blocks, dim)


def rope_tables(tokens, head_dim):
    position = jnp.arange(tokens, dtype=jnp.float32)
    freq = rope_base ** (-(jnp.arange(head_dim // 2, dtype=jnp.float32) * 2.0) / head_dim)
    angle = position[:, None] * freq[None, :]
    cos_table = jnp.concatenate([jnp.cos(angle), jnp.cos(angle)], axis=-1)
    sin_table = jnp.concatenate([jnp.sin(angle), jnp.sin(angle)], axis=-1)
    return (cos_table, sin_table)


def rotate(tensor, cos_table, sin_table):
    half = tensor.shape[-1] // 2
    turned = jnp.concatenate([-tensor[..., half:], tensor[..., :half]], axis=-1)
    return tensor * cos_table + turned * sin_table


def body(hidden, attn_gain, w_query, w_key, w_value, w_out):
    tokens = hidden.shape[0]
    head_dim = HD
    width_query = w_query.shape[1]
    width_kv = w_key.shape[1]
    kv_count = width_kv // head_dim
    group = width_query // width_kv
    x_float = hidden.astype(jnp.float32)
    inv_rms = lax.rsqrt(jnp.mean(x_float * x_float, axis=-1, keepdims=True) + norm_eps)
    grouped = sent_together((attn_gain, w_query, w_key, w_value), "rep", 0, 1)
    gain_piece, query_piece, key_piece, value_piece = sent_together(
        (grouped[0], grouped[1], grouped[2], grouped[3]), "fsdp", 0, 1
    )
    normed = (x_float * inv_rms * gain_piece.astype(jnp.float32)[None, :]).astype(jnp.bfloat16)
    queries = jnp.dot(normed, query_piece, preferred_element_type=jnp.float32)
    keys_raw = jnp.dot(normed, key_piece, preferred_element_type=jnp.float32)
    values_raw = jnp.dot(normed, value_piece, preferred_element_type=jnp.float32)
    cos_table, sin_table = rope_tables(tokens, head_dim)
    queries = queries.reshape(tokens, kv_count, group, head_dim)
    keys_raw = keys_raw.reshape(tokens, kv_count, head_dim)
    values_bf = values_raw.reshape(tokens, kv_count, head_dim).astype(jnp.bfloat16)
    rope_queries = rotate(queries, cos_table[:, None, None, :], sin_table[:, None, None, :]).astype(
        jnp.bfloat16
    )
    rope_keys = rotate(keys_raw, cos_table[:, None, :], sin_table[:, None, :]).astype(jnp.bfloat16)
    scores = jnp.einsum(
        "qkgd,skd->kgqs", rope_queries, rope_keys, preferred_element_type=jnp.float32
    ) * head_dim ** (-0.5)
    causal = jnp.arange(tokens)[:, None] >= jnp.arange(tokens)[None, :]
    scores = jnp.where(causal[None, None, :, :], scores, -1e30)
    top = jnp.max(scores, axis=-1, keepdims=True)
    expo = jnp.exp(scores - top)
    probs = (expo / jnp.sum(expo, axis=-1, keepdims=True)).astype(jnp.bfloat16)
    context = jnp.einsum("kgqs,skd->qkgd", probs, values_bf, preferred_element_type=jnp.float32)
    context = context.reshape(tokens, width_query).astype(jnp.bfloat16)
    grouped_cols = gather_directly(w_out, "rep", 1)
    branch = jnp.dot(
        context,
        lax.all_gather(grouped_cols, "fsdp", axis=1, tiled=True),
        preferred_element_type=jnp.float32,
    )
    return (x_float + branch).astype(jnp.bfloat16)


def solution(mesh):
    placed = (
        P(("fsdp", "rep"), None),
        P(("fsdp", "rep")),
        P(("fsdp", "rep"), None),
        P(("fsdp", "rep"), None),
        P(("fsdp", "rep"), None),
        P(None, ("fsdp", "rep")),
    )
    return jax.shard_map(
        body, mesh=mesh, in_specs=placed, out_specs=P(("fsdp", "rep"), None), check_vma=False
    )
```

profile of v0, /device:TPU:1, one launch (start us, length us, event | category | flops | bytes accessed | tf_op | source)
XLA Modules:
  0.0 258.1 jit_solution(10988606192208036558)
XLA Ops:
  6.5 0.0 copy-start
  6.5 0.0 all-gather.3.cloned.1.call-start
  6.5 0.8 copy.17
  7.4 0.9 concatenate.17
  8.2 17.1 %all_gather.9 = bf16[64,3073]{1,0:T(8,128)(2,1)} all-gather(bf16[8,3073]{1,0:T(8,128)(2,1)S(1)} %concatenate.17), channel_id=1, replica_groups=mesh['fsdp'=32,'rep'=8] {'rep'}, dimensions={0}, use_global_device_ids=true | all-gather | bytes 442512 | tf_op jit(solution)/shard_map/all_gather | solution.py:14
  25.4 0.0 all-gather.3.cloned.1.call-update
  25.4 0.0 all-gather.5.cloned.1.call-start
  25.4 0.8 broadcast_in_dim.12
  26.2 9.7 %all_to_all.5 = bf16[8,2048,8]{1,2,0:T(8,128)(2,1)} all-to-all(bf16[8,2048,8]{1,2,0:T(8,128)(2,1)S(1)} %broadcast_in_dim.12), channel_id=1, replica_groups=mesh['fsdp'=32,'rep'=8] {'rep'}, dimensions={0} | all-to-all | bytes 524288 | tf_op jit(solution)/shard_map/all_to_all | solution.py:24
  35.9 0.0 all-gather.5.cloned.1.call-update
  36.0 0.2 fusion.33
  36.2 0.0 copy-done
  36.2 0.3 fusion.9
  36.5 110.4 %all-gather.3.cloned.1.call-done = bf16[2048,3073]{1,0:T(8,128)(2,1)} async-done(((bf16[64,3073]{1,0:T(8,128)(2,1)}), bf16[2048,3073]{1,0:T(8,128)(2,1)}) %all-gather.3.cloned.1.call-update) | async-done | bytes 12587024 | tf_op jit(solution)/shard_map/all_gather | solution.py:14
  146.9 1.3 convert_reduce_fusion
  148.2 2.9 %fusion.19 = bf16[256,512]{1,0:T(8,128)(2,1)S(1)} fusion(bf16[2048,3073]{1,0:T(8,128)(2,1)} %all-gather.3.cloned.1.call-done, bf16[256,2048]{1,0:T(8,128)(2,1)S(1)} %copy-done, f32[2048]{0:T(1024)S(1)} %convert_reduce_fusion, f32[256]{0:T(256)S(1)} %add_rsqrt_fusion), kind=kOutput, calls=%fused_computation.26 | convolution fusion | flops 539099136 | bytes 3417088 | tf_op jit(solution)/shard_map/dot_general | solution.py:69
  151.0 0.1 copy.18
  151.2 3.7 %fusion.12 = f32[256,512]{0,1:T(8,128)S(1)} fusion(bf16[2048,3073]{1,0:T(8,128)(2,1)} %all-gather.3.cloned.1.call-done, bf16[256,2048]{1,0:T(8,128)(2,1)S(1)} %copy-done, f32[2048]{0:T(1024)S(1)} %convert_reduce_fusion, f32[256]{0:T(256)S(1)} %add_rsqrt_fusion), kind=kOutput, calls=%fused_computation.18 | convolution fusion | flops 538968064 | bytes 3679232 | tf_op jit(solution)/shard_map/dot_general | solution.py:68
  154.9 10.6 %fusion.1 = f32[256,2048]{0,1:T(8,128)S(1)} fusion(bf16[2048,3073]{1,0:T(8,128)(2,1)} %all-gather.3.cloned.1.call-done, bf16[256,2048]{1,0:T(8,128)(2,1)S(1)} %copy-done, f32[2048]{0:T(1024)S(1)} %convert_reduce_fusion, f32[256]{0:T(256)S(1)} %add_rsqrt_fusion), kind=kOutput, calls=%fused_computation.1 | convolution fusion | flops 2149580800 | bytes 11543552 | tf_op jit(solution)/shard_map/dot_general | solution.py:67
  165.5 0.2 slice_negate_fusion
  165.7 1.5 fusion.22
  167.2 2.3 fusion.40
  169.5 0.9 fusion.18
  170.4 74.1 %all-gather.5.cloned.1.call-done = bf16[2048,2048]{0,1:T(8,128)(2,1)} async-done(((bf16[2048,64]{0,1:T(8,128)(2,1)}), bf16[2048,2048]{0,1:T(8,128)(2,1)}) %all-gather.5.cloned.1.call-update) | async-done | bytes 8388624 | tf_op jit(solution)/shard_map/all_gather | solution.py:91
  244.5 6.7 %fusion.8 = bf16[256,2048]{1,0:T(8,128)(2,1)} fusion(bf16[256,2048]{0,1:T(8,128)(2,1)S(1)} %bitcast.40, bf16[2048,2048]{0,1:T(8,128)(2,1)} %all-gather.5.cloned.1.call-done, bf16[256,2048]{1,0:T(8,128)(2,1)S(1)} %copy-done), kind=kOutput, calls=%fused_computation.14 | convolution fusion | flops 2149056512 | bytes 11534336 | tf_op jit(solution)/shard_map/dot_general | solution.py:89
  (5 shorter events, 0.1 us)
Async XLA Ops:
  6.5 29.7 %copy-start = (bf16[256,2048]{1,0:T(8,128)(2,1)S(1)}, bf16[256,2048]{1,0:T(8,128)(2,1)}, u32[]{:S(2)}) copy-start(bf16[256,2048]{1,0:T(8,128)(2,1)} %param.6) | copy-start | bytes 3145732
  6.5 140.4 %all-gather.3.cloned.1.call-start = ((), (), s32[]{:S(2)}) async-start(), calls=%async_computation.1 | async-start | bytes 13516800 | tf_op jit(solution)/shard_map/all_gather | solution.py:14
  25.4 219.1 %all-gather.5.cloned.1.call-start = ((), (), s32[]{:S(2)}) async-start(), calls=%async_computation.2 | async-start | bytes 8650752 | tf_op jit(solution)/shard_map/all_gather | solution.py:91
Sparse Core Ops, SparseCore 0:
  25.5 121.3 all-gather.2
  149.5 94.9 all-gather.4
where the time goes:
time: 258 us
  waiting for transfers between devices  184 us (71%)
  blocking collectives  26.8 us (10%)
  matrix products  26.3 us (10%)
  between operations  13.5 us (5%)
  other arithmetic  4.28 us (2%)
  local copies, waits for them, and re-layouts  2.62 us (1%)
    all_gather x1, waiting for transfers between devices, sent_together(): lax.all_gather(both, axis, axis=dim, tiled=True)  110 us
    all_gather x1, waiting for transfers between devices, body(): lax.all_gather(grouped_cols, 'fsdp', axis=1, tiled=True)  74.1 us
    all_gather x1, blocking collectives, sent_together(): lax.all_gather(both, axis, axis=dim, tiled=True)  17.1 us
    dot_general x1, matrix products, body(): queries = jnp.dot(normed, query_piece, preferred_element_type=jnp.float32)  10.6 us
    all_to_all x1, blocking collectives, copy_for_each(): return lax.all_to_all(copies, axis, split_axis=0, concat_axis=0, tiled=True)  9.7 us
    dot_general x1, matrix products, body(): jnp.dot(context, lax.all_gather(grouped_cols, 'fsdp', axis=1, tiled=True)...  6.74 us
  transfers between devices with their start and end apart: 2, of which 2 were waited for; matrix products, arithmetic and copies ran while one was open for 10% of the time, Pallas kernels for 0%

commit v1 on v0

--- a/solution.py
+++ b/solution.py
@@ -6,6 +6,11 @@
 HD = 64
 rope_base = 500000.0
 norm_eps = 1e-05
+
+
+def all_by_exchange(array, mesh_axis, d):
+    stack = jnp.stack([array] * lax.axis_size(mesh_axis))
+    return jnp.concatenate(lax.all_to_all(stack, mesh_axis, 0, 0), axis=d)
 
 
 def sent_together(arrays, axis, dim, along):
@@ -87,9 +92,7 @@
     context = context.reshape(tokens, width_query).astype(jnp.bfloat16)
     grouped_cols = gather_directly(w_out, "rep", 1)
     branch = jnp.dot(
-        context,
-        lax.all_gather(grouped_cols, "fsdp", axis=1, tiled=True),
-        preferred_element_type=jnp.float32,
+        context, all_by_exchange(grouped_cols, "fsdp", 1), preferred_element_type=jnp.float32
     )
     return (x_float + branch).astype(jnp.bfloat16)
 

time: 258 us -> 340 us (1.32); the launches traced: 258 us -> 335 us
  waiting for transfers between devices: 184 us -> 247 us
  starting transfers between devices: 0.04 us -> 11.1 us
  local copies, waits for them, and re-layouts: 2.62 us -> 6.85 us
    all_gather x1, waiting for transfers between devices: 110 us -> 247 us  [sent_together(): lax.all_gather(both, axis, axis=dim, tiled=True)]
    all_gather x1 -> x0, waiting for transfers between devices: 74.1 us -> none  [body(): lax.all_gather(grouped_cols, 'fsdp', axis=1, tiled=True)]
    all_to_all x0 -> x1, starting transfers between devices: none -> 11.1 us  [all_by_exchange(): return jnp.concatenate(lax.all_to_all(stack, mesh_axis, 0, 0), axis=d)]
    another operation x0 -> x1, local copies, waits for them, and re-layouts: none -> 4.32 us  [all_by_exchange(): stack = jnp.stack([array] * lax.axis_size(mesh_axis))]
  transfers between devices with their start and end apart: 2 -> 2, of which waited for: 2 -> 1; matrix products, arithmetic and copies ran while one was open for 10% -> 9% of each run, Pallas kernels for 0% -> 0%
where the time goes in v1:
time: 340 us; the launch traced here: 335 us
  waiting for transfers between devices  247 us (73%)
  blocking collectives  26.3 us (8%)
  matrix products  26.3 us (8%)
  between operations  13.5 us (4%)
  starting transfers between devices  11.1 us (3%)
  local copies, waits for them, and re-layouts  6.85 us (2%)
  other arithmetic  4.28 us (1%)
    all_gather x1, waiting for transfers between devices, sent_together(): lax.all_gather(both, axis, axis=dim, tiled=True)  247 us
    all_gather x1, blocking collectives, sent_together(): lax.all_gather(both, axis, axis=dim, tiled=True)  17.1 us
    all_to_all x1, starting transfers between devices, all_by_exchange(): return jnp.concatenate(lax.all_to_all(stack, mesh_axis, 0, 0), axis=d)  11.1 us
    dot_general x1, matrix products, body(): queries = jnp.dot(normed, query_piece, preferred_element_type=jnp.float32)  10.6 us
    all_to_all x1, blocking collectives, copy_for_each(): return lax.all_to_all(copies, axis, split_axis=0, concat_axis=0, tiled=True)  9.16 us
  transfers between devices with their start and end apart: 2, of which 1 were waited for; matrix products, arithmetic and copies ran while one was open for 9% of the time, Pallas kernels for 0%

profile of v1, /device:TPU:1, one launch (start us, length us, event | category | flops | bytes accessed | tf_op | source)
XLA Modules:
  0.0 335.4 jit_solution(2032995712337194645)
XLA Ops:
  6.5 0.0 all-gather.2.cloned.1.call-start
  6.5 0.7 copy.17
  7.3 0.9 concatenate.17
  8.2 17.1 %all_gather.6 = bf16[64,3073]{1,0:T(8,128)(2,1)} all-gather(bf16[8,3073]{1,0:T(8,128)(2,1)S(1)} %concatenate.17), channel_id=1, replica_groups=mesh['fsdp'=32,'rep'=8] {'rep'}, dimensions={0}, use_global_device_ids=true | all-gather | bytes 442512 | tf_op jit(solution)/shard_map/all_gather | solution.py:19
  25.3 0.0 all-gather.2.cloned.1.call-update
  25.3 0.8 broadcast_in_dim.12
  26.1 9.2 %all_to_all.10 = bf16[8,2048,8]{1,2,0:T(8,128)(2,1)S(1)} all-to-all(bf16[8,2048,8]{1,2,0:T(8,128)(2,1)S(1)} %broadcast_in_dim.12), channel_id=1, replica_groups=mesh['fsdp'=32,'rep'=8] {'rep'}, dimensions={0} | all-to-all | bytes 524288 | tf_op jit(solution)/shard_map/all_to_all | solution.py:29
  35.2 4.3 %stack.3 = bf16[32,2048,64]{1,2,0:T(8,128)(2,1)} broadcast(bf16[2048,64]{0,1:T(8,128)(2,1)S(1)} %bitcast.40), dimensions={1,2} | broadcast | bytes 8650752 | tf_op jit(solution)/shard_map/stack | solution.py:12
  39.6 0.0 copy-start
  39.6 11.1 %all-to-all-start.1 = ((bf16[32,2048,64]{1,2,0:T(8,128)(2,1)}), bf16[32,2048,64]{1,2,0:T(8,128)(2,1)}, u32[]{:S(2)}, u32[]{:S(2)}) async-start(bf16[32,2048,64]{1,2,0:T(8,128)(2,1)} %stack.3), calls=%async_computation.1 | async-start | bytes 16777216 | tf_op jit(solution)/shard_map/all_to_all | solution.py:13
  50.7 0.2 fusion.33
  50.9 0.0 copy-done
  50.9 0.3 fusion.9
  51.2 247.1 %all-gather.2.cloned.1.call-done = bf16[2048,3073]{1,0:T(8,128)(2,1)} async-done(((bf16[64,3073]{1,0:T(8,128)(2,1)}), bf16[2048,3073]{1,0:T(8,128)(2,1)}) %all-gather.2.cloned.1.call-update) | async-done | bytes 12587024 | tf_op jit(solution)/shard_map/all_gather | solution.py:19
  298.3 1.3 convert_reduce_fusion
  299.6 2.9 fusion.19
  302.5 0.1 copy.18
  302.6 3.7 %fusion.12 = f32[256,512]{0,1:T(8,128)S(1)} fusion(bf16[2048,3073]{1,0:T(8,128)(2,1)} %all-gather.2.cloned.1.call-done, bf16[256,2048]{1,0:T(8,128)(2,1)S(1)} %copy-done, f32[2048]{0:T(1024)S(1)} %convert_reduce_fusion, f32[256]{0:T(256)S(1)} %add_rsqrt_fusion), kind=kOutput, calls=%fused_computation.18 | convolution fusion | flops 538968064 | bytes 3679232 | tf_op jit(solution)/shard_map/dot_general | solution.py:73
  306.4 10.6 %fusion.1 = f32[256,2048]{0,1:T(8,128)S(1)} fusion(bf16[2048,3073]{1,0:T(8,128)(2,1)} %all-gather.2.cloned.1.call-done, bf16[256,2048]{1,0:T(8,128)(2,1)S(1)} %copy-done, f32[2048]{0:T(1024)S(1)} %convert_reduce_fusion, f32[256]{0:T(256)S(1)} %add_rsqrt_fusion), kind=kOutput, calls=%fused_computation.1 | convolution fusion | flops 2149580800 | bytes 11543552 | tf_op jit(solution)/shard_map/dot_general | solution.py:72
  317.0 0.2 slice_negate_fusion
  317.1 1.5 fusion.22
  318.6 2.3 fusion.40
  320.9 0.9 fusion.18
  321.8 0.0 all-to-all-done.1
  321.8 6.7 %fusion.8 = bf16[256,2048]{1,0:T(8,128)(2,1)} fusion(bf16[256,2048]{0,1:T(8,128)(2,1)S(1)} %bitcast.43, bf16[2048,2048]{0,1:T(8,128)(2,1)} %bitcast.14, bf16[256,2048]{1,0:T(8,128)(2,1)S(1)} %copy-done), kind=kOutput, calls=%fused_computation.14 | convolution fusion | flops 2149056512 | bytes 11534336 | tf_op jit(solution)/shard_map/dot_general | solution.py:94
  (5 shorter events, 0.1 us)
Async XLA Ops:
  6.5 291.8 %all-gather.2.cloned.1.call-start = ((), (), s32[]{:S(2)}) async-start(), calls=%async_computation.2 | async-start | bytes 13516800 | tf_op jit(solution)/shard_map/all_gather | solution.py:19
  39.6 11.3 %copy-start = (bf16[256,2048]{1,0:T(8,128)(2,1)S(1)}, bf16[256,2048]{1,0:T(8,128)(2,1)}, u32[]{:S(2)}) copy-start(bf16[256,2048]{1,0:T(8,128)(2,1)} %param.6) | copy-start | bytes 3145732
  39.6 282.3 %all-to-all-start.1 = ((bf16[32,2048,64]{1,2,0:T(8,128)(2,1)}), bf16[32,2048,64]{1,2,0:T(8,128)(2,1)}, u32[]{:S(2)}, u32[]{:S(2)}) async-start(bf16[32,2048,64]{1,2,0:T(8,128)(2,1)} %stack.3), calls=%async_computation.1 | async-start | bytes 16777216 | tf_op jit(solution)/shard_map/all_to_all | solution.py:13
Sparse Core Ops, SparseCore 0:
  25.4 272.8 all-gather.1
